TPU v7x, 32 devices: a whole 2x2x4 slice. The times are simulated.
32 devices in a mesh: grid: 16 (over z, x, core), member: 2 (over y).
Axes of the slice: x: 2, y: 2, z: 4, core: 2. Of those that a mesh axis runs over, the one named last changes fastest.
Arguments:
- fields: bfloat16 [2, 16384, 1024], P('member', 'grid'), may hold values from -0.796875 to 0.796875
- observed: bfloat16 [100, 16384], P(None, 'grid'), may hold values from -6 to 6
- lat_weight: float32 [16384], P('grid'), may hold values from 0.3 to 6, as said below
- var_weight: float32 [100], replicated, may hold values from 0.25 to 4
- weight: bfloat16 [100, 1024], replicated, may hold values from -0.1875 to 0.1875
- bias: float32 [100], replicated, may hold values from -1 to 1
- gain: float32 [1024], replicated, may hold values from 0.1 to 1.9
Outputs:
- grad_fields: bfloat16 [2, 16384, 1024], P('member', 'grid')
- grad_weight: float32 [100, 1024], replicated
- grad_gain: float32 [1024], replicated
- grad_bias: float32 [100], replicated
- loss: float32 [], replicated
Inputs may be any that keep to these rules, and one draw needn't show every extreme that they name: `lat_weight`: positive.
All inputs are finite; a program needn't handle non-finite values.
Results may differ from a plain program's by a relative error of at most 0.0014.
The roundings to bfloat16 on the way count: a program that leaves them out, or rounds other values in their place, can miss the bound.
Values sent between devices are 32-bit elements; how exact they have to be, the bound alone decides.
A program may use at most 64 MiB of HBM per device.

v0:
```python
import jax
import jax.numpy as jnp
from jax import lax
from jax.sharding import PartitionSpec as P

soft_square = 0.01
norm_epsilon = 1e-05


def normalize(member_rows, gain):
    values = member_rows.astype(jnp.float32)
    row_mean = jnp.mean(values, axis=-1, keepdims=True)
    centred = values - row_mean
    inv_std = lax.rsqrt(jnp.mean(centred * centred, axis=-1, keepdims=True) + norm_epsilon)
    unit_rows = centred * inv_std
    normed = (unit_rows * gain[None, None, :]).astype(jnp.bfloat16)
    return (normed, unit_rows, inv_std)


def shards(fields, observed, lat_weight, var_weight, weight, bias, gain):
    own_rows = fields.shape[0]
    local_points = fields.shape[1]
    members = own_rows * lax.axis_size("member")
    normed, unit_rows, inv_std = normalize(fields, gain)
    predicted = (
        jnp.einsum("vd,rpd->rvp", weight, normed, preferred_element_type=jnp.float32)
        + bias[None, :, None]
    )
    lat_total = lax.psum(jnp.sum(lat_weight), "grid")
    target = observed.astype(jnp.float32)
    obs_gap = predicted - target[None]
    obs_abs = jnp.sqrt(obs_gap * obs_gap + soft_square)
    obs_sign = obs_gap / obs_abs
    weight_grid = var_weight[:, None] * lat_weight[None, :]
    scale_pair = 1.0 / (members * (members - 1))
    everyone = lax.all_gather(predicted, "member", axis=0, tiled=True)
    gap = predicted[:, None] - everyone[None]
    soft_abs = jnp.sqrt(gap * gap + soft_square)
    pair_sign = jnp.sum(gap / soft_abs, axis=1)
    first_rows = lax.axis_index("member") * own_rows + jnp.arange(own_rows, dtype=jnp.int32)
    upper = (jnp.arange(members, dtype=jnp.int32)[None, :] > first_rows[:, None]).astype(
        jnp.float32
    )
    pair_abs = jnp.sum(soft_abs * upper[:, :, None, None], axis=(0, 1))
    pair_loss = jnp.sum(pair_abs * weight_grid)
    obs_loss = jnp.sum(jnp.sum(obs_abs, axis=0) * weight_grid)
    loss_part = obs_loss / members - pair_loss * scale_pair
    grad_pred = (weight_grid[None] * (obs_sign / members - pair_sign * scale_pair)).astype(
        jnp.bfloat16
    )
    points_total = local_points * lax.axis_size("grid")
    factor = points_total / lat_total
    grad_normed = jnp.einsum("rvp,vd->rpd", grad_pred, weight, preferred_element_type=jnp.float32)
    grad_unit = grad_normed * gain[None, None, :]
    mean_one = jnp.mean(grad_unit, axis=-1, keepdims=True)
    mean_two = jnp.mean(grad_unit * unit_rows, axis=-1, keepdims=True)
    grad_fields = (factor * (inv_std * (grad_unit - mean_one - unit_rows * mean_two))).astype(
        jnp.bfloat16
    )
    part_weight = jnp.einsum("rvp,rpd->vd", grad_pred, normed, preferred_element_type=jnp.float32)
    part_gain = jnp.sum(grad_normed * unit_rows, axis=(0, 1))
    part_bias = jnp.sum(grad_pred.astype(jnp.float32), axis=(0, 2))
    grad_weight, grad_gain, grad_bias, loss_total = lax.psum(
        (part_weight, part_gain, part_bias, loss_part), ("grid", "member")
    )
    variables = observed.shape[0]
    loss = loss_total / (variables * lat_total)
    return (grad_fields, factor * grad_weight, factor * grad_gain, factor * grad_bias, loss)


def solution(mesh):
    return jax.shard_map(
        shards,
        mesh=mesh,
        in_specs=(P("member", "grid", None), P(None, "grid"), P("grid"), P(), P(), P(), P()),
        out_specs=(P("member", "grid", None), P(), P(), P(), P()),
        check_vma=False,
    )
```

profile of v0, /device:TPU:1, one launch (start us, length us, event | category | flops | bytes accessed | tf_op | source)
XLA Modules:
  0.0 166.7 jit_solution(458658139625485264)
XLA Ops:
  7.2 0.0 copy-start
  7.2 0.0 all-reduce.3.cloned.1.call-start
  7.3 2.9 %copy.14 = bf16[1,1024,1024]{1,2,0:T(8,128)(2,1)S(1)} copy(bf16[1,1024,1024]{2,1,0:T(8,128)(2,1)} %param.7) | data formatting | bytes 4194304 | tf_op args[0]
  10.2 0.4 convert_reduce_fusion
  10.5 0.6 fusion.13
  11.2 0.8 fusion.15
  12.0 12.3 %all_gather.3 = f32[2,100,1024]{2,1,0:T(8,128)S(1)} all-gather(f32[1,100,1024]{2,1,0:T(8,128)S(1)} %bitcast.43), channel_id=1, replica_groups=mesh['grid'=16,'member'=2] {'member'}, dimensions={0}, use_global_device_ids=true | all-gather | bytes 1228800 | tf_op jit(solution)/shard_map/all_gather | solution.py:36
  24.3 0.6 multiply_reduce_fusion.1
  24.9 0.4 convert_reduce_fusion.1
  25.3 0.7 copy-done.2
  26.0 1.7 fusion.20
  27.6 0.0 all-reduce.3.cloned.1.call-update
  27.6 0.6 reduce_sum.105
  28.2 4.2 %fusion.12 = (f32[1024]{0:T(1024)S(1)}, f32[1024]{0:T(1024)S(1)}, f32[1024,1024]{0,1:T(8,128)}) fusion(bf16[1,1024,1024]{1,2,0:T(8,128)(2,1)S(1)} %copy.14, f32[1024]{0:T(1024)S(1)} %add_rsqrt_fusion, f32[1024]{0:T(1024)S(1)} %broadcast_multiply_fusion.4, f32[1024]{0:T(1024)S(1)} %copy-done.4, bf16[100,1024]{1,0:T(8,128)(2,1)S(1)} %copy-done, ...), kind=kOutput, calls=%fused_computation.14 | convolution fusion | flops 218101760 | bytes 6721536 | tf_op jit(solution)/shard_map/rvp,vd->rpd/dot_general | solution.py:53
  32.5 31.2 %psum.35 = f32[]{:T(128)} all-reduce(f32[]{:T(128)} %reduce_sum.105), channel_id=1, replica_groups=mesh['grid'=16,'member'=2] {'grid'}, use_global_device_ids=true, to_apply=%region_1.0 | all-reduce | flops 1 | bytes 8 | tf_op jit(solution)/shard_map/psum | solution.py:29
  65.0 1.0 fusion.17
  67.3 2.6 %multiply_reduce_fusion = f32[1024]{0:T(1024)S(1)} fusion(f32[1024,1024]{0,1:T(8,128)} %get-tuple-element.26, f32[1024]{0:T(1024)S(1)} %copy-done.4), kind=kLoop, calls=%fused_computation.16 | loop fusion | flops 2096128 | bytes 4202496 | tf_op jit(solution)/shard_map/reduce_sum | solution.py:55
  69.9 39.6 %all-reduce = (f32[1024]{0:T(1024)S(1)}, f32[100]{0:T(128)S(1)}, f32[]{:T(128)}) all-reduce(f32[1024]{0:T(1024)S(1)} %get-tuple-element.15, f32[100]{0:T(128)S(1)} %get-tuple-element.24, f32[]{:T(128)S(6)} %sub.53), channel_id=1, replica_groups=mesh['grid'=16,'member'=2] {'grid','member'}, use_global_device_ids=true, to_apply=%region_9.0 | all-reduce | flops 1125 | bytes 9000 | tf_op jit(solution)/shard_map/psum | solution.py:63
  109.5 0.6 broadcast_multiply_fusion.1
  110.1 4.8 %fusion.11 = bf16[1,1024,1024]{1,2,0:T(8,128)(2,1)} fusion(bf16[1,1024,1024]{1,2,0:T(8,128)(2,1)S(1)} %copy.14, f32[1024,1024]{0,1:T(8,128)} %get-tuple-element.26, f32[1024]{0:T(1024)S(1)} %broadcast_multiply_fusion.2, f32[1024]{0:T(1024)S(1)} %broadcast_multiply_fusion.3, f32[1024]{0:T(1024)S(1)} %copy-done.4, f32[1024]{0:T(1024)S(1)} %add_rsqrt_fusion, ...), kind=kLoop, calls=%fused_computation.13 | loop fusion | flops 10485760 | bytes 8409092 | tf_op jit(solution)/shard_map/convert_element_type | solution.py:57
  114.9 3.9 %copy.15 = bf16[1,1024,1024]{2,1,0:T(8,128)(2,1)} copy(bf16[1,1024,1024]{1,2,0:T(8,128)(2,1)} %fusion.11) | data formatting | bytes 4194304
  119.5 0.5 broadcast_multiply_fusion.5
  120.0 36.9 %all-reduce.3.cloned.1.call-done = f32[100,1024]{1,0:T(8,128)} async-done(((f32[100,1024]{1,0:T(8,128)}), f32[100,1024]{1,0:T(8,128)}) %all-reduce.3.cloned.1.call-update) | async-done | bytes 409616 | tf_op jit(solution)/shard_map/psum | solution.py:63
  156.9 1.8 %broadcast_multiply_fusion = f32[100,1024]{1,0:T(8,128)} fusion(f32[100,1024]{1,0:T(8,128)} %all-reduce.3.cloned.1.call-done, f32[]{:T(128)S(6)} %div.36), kind=kLoop, calls=%fused_computation.37 | loop fusion | flops 102400 | bytes 819204 | tf_op jit(solution)/shard_map/mul | solution.py:68
  (17 shorter events, 0.1 us)
Async XLA Ops:
  7.2 4.0 %copy-start = (bf16[100,1024]{1,0:T(8,128)(2,1)S(1)}, bf16[100,1024]{1,0:T(8,128)(2,1)}, u32[]{:S(2)}) copy-start(bf16[100,1024]{1,0:T(8,128)(2,1)} %param.11) | copy-start | bytes 614404
  7.2 149.7 %all-reduce.3.cloned.1.call-start = ((), (), s32[]{:S(2)}) async-start(), calls=%async_computation | async-start | bytes 851968 | tf_op jit(solution)/shard_map/psum | solution.py:63
  7.2 3.9 %copy-start.4 = (f32[1024]{0:T(1024)S(1)}, f32[1024]{0:T(1024)}, u32[]{:S(2)}) copy-start(f32[1024]{0:T(1024)} %param.13) | copy-start | bytes 12292
  7.3 3.9 %copy-start.6 = (f32[100]{0:T(128)S(1)}, f32[100]{0:T(128)}, u32[]{:S(2)}) copy-start(f32[100]{0:T(128)} %param.12) | copy-start | bytes 1204
  11.2 13.7 %copy-start.1 = (bf16[100,1024]{1,0:T(8,128)(2,1)S(1)}, bf16[100,1024]{1,0:T(8,128)(2,1)}, u32[]{:S(2)}) copy-start(bf16[100,1024]{1,0:T(8,128)(2,1)} %param.8) | copy-start | bytes 614404
  11.2 13.7 %copy-start.3 = (f32[1024]{0:T(1024)S(1)}, f32[1024]{0:T(1024)}, u32[]{:S(2)}) copy-start(f32[1024]{0:T(1024)} %param.9) | copy-start | bytes 12292
  11.2 13.7 %copy-start.5 = (f32[100]{0:T(128)S(1)}, f32[100]{0:T(128)}, u32[]{:S(2)}) copy-start(f32[100]{0:T(128)} %param.10) | copy-start | bytes 1204
  25.3 0.7 copy-start.2
Sparse Core Ops, SparseCore 0:
  27.8 129.1 all-reduce.2
where the time goes:
time: 168 us; the launch traced here: 167 us
  blocking collectives  83.1 us (49%)
  waiting for transfers between devices  36.9 us (22%)
  between operations  18.6 us (11%)
  other arithmetic  13.8 us (8%)
  local copies, waits for them, and re-layouts  7.56 us (4%)
  matrix products  6.7 us (4%)
    psum x1, blocking collectives, shards(): lax.psum((part_weight, part_gain, part_bias, loss_part), ('grid', 'member'))  39.6 us
    psum x1, waiting for transfers between devices, shards(): lax.psum((part_weight, part_gain, part_bias, loss_part), ('grid', 'member'))  36.9 us
    psum x1, blocking collectives, shards(): lat_total = lax.psum(jnp.sum(lat_weight), 'grid')  31.2 us
    all_gather x1, blocking collectives, shards(): everyone = lax.all_gather(predicted, 'member', axis=0, tiled=True)  12.3 us
    unnamed x16, local copies, waits for them, and re-layouts  7.56 us
    convert_element_type x1, other arithmetic, shards(): (factor * (inv_std * (grad_unit - mean_one - unit_rows * mean_two))).asty...  4.84 us
    dot_general x1, matrix products, shards(): jnp.einsum('rvp,vd->rpd', grad_pred, weight, preferred_element_type=jnp.f...  4.23 us
  transfers between devices with their start and end apart: 1, of which 1 were waited for; matrix products, arithmetic and copies ran while one was open for 11% of the time, Pallas kernels for 0%

commit v1 on v0

v1 whole, which is shorter than its diff:
```python
import functools

import jax
import jax.numpy as jnp
from jax import lax
from jax.experimental import pallas as pl
from jax.experimental.pallas import tpu as pltpu
from jax.sharding import PartitionSpec as P

soft_square = 0.01
norm_epsilon = 1e-05
LANES = 128
ROW_CHUNKS = 4
POINT_BLOCK = 128
NORM_ROWS = 64
f32 = jnp.float32
bf16 = jnp.bfloat16
MESH_ID = pl.DeviceIdType.MESH


def plan(G, M, V, D):
    K = ROW_CHUNKS
    offs = [int(V * k / K / 16 + 0.5) * 16 for k in range(K)] + [V]
    rows = [offs[k + 1] - offs[k] for k in range(K)]
    extra = -(-(rows[-1] + 2) // 8) * 8
    blocks = rows[:-1] + [extra]
    C = D // LANES
    per = G // K
    S = (M * per) // C
    assert G % K == 0 and (M * per) % C == 0 and S >= 1
    return K, offs, rows, blocks, C, per, S


def to_column(row, size):
    r = lax.broadcasted_iota(jnp.int32, (size, row.shape[1]), 0)
    c = lax.broadcasted_iota(jnp.int32, (size, row.shape[1]), 1)
    return jnp.sum(jnp.where(r == c, row, 0.0), axis=1, keepdims=True)


def body(G, M, fields, obs, lat, vw, w, bias, gain,
         gf, gw, gg, gb, loss,
         x, unit, normed, inv, outb, wp, gp, pred, others, lat_own, lat_all,
         part, rs, ag_src, ag, lossb,
         in_sem, out_sem, lat_send, lat_recv, ps_first, pr_first, ps, pr,
         rs_send, rs_recv, ag_send, ag_recv):
    V, PTS = obs.shape
    D = w.shape[1]
    VP = wp.shape[0]
    N = G * M
    K, offs, rows, blocks, C, per, S = plan(G, M, V, D)
    ends = [-(-hi // 8) * 8 for hi in offs[1:]]
    J = PTS // POINT_BLOCK
    g = lax.axis_index("grid")
    m = lax.axis_index("member")
    me = m * G + g
    my_k = lax.rem(g, K)
    my_cf = m * per + g // K
    my_c = my_cf // S

    def device(t):
        return {"grid": lax.rem(t, G), "member": t // G}

    barrier = pltpu.get_barrier_semaphore()

    @pl.loop(1, N)
    def _(i):
        pl.semaphore_signal(barrier, inc=1, device_id=device(lax.rem(me + i, N)), device_id_type=MESH_ID)

    def load(j):
        at = pl.ds(pl.multiple_of(j * POINT_BLOCK, POINT_BLOCK), POINT_BLOCK)
        return pltpu.make_async_copy(fields.at[0, at], x.at[at], in_sem.at[j])

    for j in range(J):
        load(j).start()
    wp[...] = jnp.zeros(wp.shape, bf16)
    wp[0:V, :] = w[...]
    gp[...] = jnp.zeros(gp.shape, bf16)
    lat_own[...] = jnp.full(lat_own.shape, jnp.sum(lat[...]), f32)
    bias_col = to_column(bias[...], VP)
    vw_col = to_column(vw[...], VP)
    gain_row = gain[...]
    pl.semaphore_wait(barrier, N - 1)

    def lat_copy(i):
        return pltpu.make_async_remote_copy(
            lat_own, lat_all.at[g], lat_send.at[i], lat_recv.at[g],
            device_id={"grid": lax.rem(g + i, G), "member": m}, device_id_type=MESH_ID)

    @pl.loop(1, G)
    def _(i):
        lat_copy(i).start()

    def pred_copy(i, k, at, send, recv):
        return pltpu.make_async_remote_copy(
            pred.at[offs[k]:ends[k], at], others.at[i, offs[k]:ends[k], at], send, recv,
            device_id={"grid": g, "member": lax.rem(m + i, M)}, device_id_type=MESH_ID)

    def points(j):
        return pl.ds(pl.multiple_of(j * POINT_BLOCK, POINT_BLOCK), POINT_BLOCK)

    @pl.loop(0, J)
    def _(j):
        load(j).wait()
        for b in range(POINT_BLOCK // NORM_ROWS):
            at = pl.ds(pl.multiple_of(j * POINT_BLOCK + b * NORM_ROWS, NORM_ROWS), NORM_ROWS)
            values = x[at, :].astype(f32)
            centred = values - jnp.mean(values, axis=-1, keepdims=True)
            istd = lax.rsqrt(jnp.mean(centred * centred, axis=-1, keepdims=True) + norm_epsilon)
            u = centred * istd
            unit[at, :] = u
            inv[at, :] = istd
            normed[at, :] = (u * gain_row).astype(bf16)
        p = lax.dot_general(wp[...], normed[points(j), :], (((1,), (1,)), ((), ())),
                            preferred_element_type=f32)
        pred[:, points(j)] = p + bias_col
        for i in range(1, M):
            pred_copy(i, 0, points(j), ps_first.at[i, j], pr_first.at[i, j]).start()

    whole = slice(0, PTS)
    for k in range(1, K):
        for i in range(1, M):
            pred_copy(i, k, whole, ps.at[i, k], pr.at[i, k]).start()

    lat_all[g] = lat_own[...]

    @pl.loop(1, G)
    def _(i):
        src = lax.rem(g + i, G)
        pltpu.make_async_copy(lat_own, lat_all.at[src], lat_recv.at[src]).wait()

    lat_total = jnp.sum(lat_all[...], axis=0)[0:1, 0:1]
    factor = (PTS * G) / lat_total

    scale_pair = 1.0 / (M * (M - 1))
    lossb[...] = jnp.zeros(lossb.shape, f32)
    ones = jnp.ones((8, PTS), bf16)

    def unit_device(k, c):
        cf = c * S
        return cf // per, (cf % per) * K + k

    def rs_copy(k, c):
        om, og = unit_device(k, c)
        return pltpu.make_async_remote_copy(
            part.at[k, c, 0:blocks[k]], rs.at[me, 0:blocks[k]], rs_send.at[k, c], rs_recv.at[me],
            device_id={"grid": og, "member": om}, device_id_type=MESH_ID)

    def not_mine(k, c):
        om, og = unit_device(k, c)
        return jnp.logical_or(m != om, g != og)

    for k in range(K):
        for i in range(1, M):
            if k == 0:
                for j in range(J):
                    pred_copy(i, 0, points(j), ps_first.at[i, j], pr_first.at[i, j]).wait_recv()
            else:
                pred_copy(i, k, whole, ps.at[i, k], pr.at[i, k]).wait_recv()
        lo, hi, R = offs[k], offs[k + 1], rows[k]
        own = pred[lo:hi, :]
        e = own - obs[lo:hi, :].astype(f32)
        sq = e * e + soft_square
        r = lax.rsqrt(sq)
        grad = e * r * (1.0 / M)
        crps = sq * r * (1.0 / M)
        for i in range(1, M):
            e = own - others[i, lo:hi, :]
            sq = e * e + soft_square
            r = lax.rsqrt(sq)
            grad = grad - e * r * scale_pair
            crps = crps - sq * r * (0.5 * scale_pair)
        wg = vw_col[lo:hi, :] * lat[...]
        gk = (wg * grad).astype(bf16)
        lossb[...] += jnp.sum(wg * crps, axis=0, keepdims=True)
        gp[lo:hi, :] = gk
        gwk = jnp.dot(gk, normed[...], preferred_element_type=f32)
        if k == K - 1:
            gbp = lax.dot_general(ones, gp[...], (((1,), (1,)), ((), ())), preferred_element_type=f32)
            lane = jnp.zeros((1, LANES), f32)
            for j in range(PTS // LANES):
                lane = lane + lossb[:, j * LANES:(j + 1) * LANES]
        for c in range(C):
            part[k, c, 0:R] = gwk[:, c * LANES:(c + 1) * LANES]
            if k == K - 1:
                part[k, c, R:R + 1] = gbp[0:1, :]
                part[k, c, R + 1:R + 2] = lane
                if blocks[k] > R + 2:
                    part[k, c, R + 2:blocks[k]] = jnp.zeros((blocks[k] - R - 2, LANES), f32)
        for c in range(C):
            @pl.when(not_mine(k, c))
            def _(k=k, c=c):
                rs_copy(k, c).start()

    def ag_copy(k, i):
        B = blocks[k]
        return pltpu.make_async_remote_copy(
            ag_src.at[0:B], ag.at[k, my_c, 0:B], ag_send.at[i], ag_recv.at[k, my_c],
            device_id=device(lax.rem(me + i, N)), device_id_type=MESH_ID)

    is_owner = lax.rem(my_cf, S) == 0

    def reduce_and_spread(k):
        B = blocks[k]

        @pl.when(jnp.logical_and(is_owner, my_k == k))
        def _():
            def add(i, acc):
                src = lax.rem(me + i, N)
                pltpu.make_async_copy(part.at[k, 0, 0:B], rs.at[src, 0:B], rs_recv.at[src]).wait()
                return acc + rs[src, 0:B]

            acc = lax.fori_loop(1, N, add, part[k, my_c, 0:B]) * factor
            ag_src[0:B] = acc
            ag[k, my_c, 0:B] = acc

            @pl.loop(1, N)
            def _(i):
                ag_copy(k, i).start()

    def out_copy(j):
        return pltpu.make_async_copy(outb.at[points(j)], gf.at[0, points(j)], out_sem.at[j])

    def grad_block(j):
        gn = lax.dot_general(gp[:, points(j)], wp[...], (((0,), (0,)), ((), ())),
                             preferred_element_type=f32)
        gu = gn * gain_row
        u = unit[points(j), :]
        one = jnp.mean(gu, axis=-1, keepdims=True)
        two = jnp.mean(gu * u, axis=-1, keepdims=True)
        outb[points(j), :] = ((factor * inv[points(j), :]) * (gu - one - u * two)).astype(bf16)
        out_copy(j).start()

    for k in range(K - 2):
        reduce_and_spread(k)
    pl.loop(0, J // 2)(grad_block)
    for k in range(K - 2, K):
        reduce_and_spread(k)
    pl.loop(J // 2, J)(grad_block)

    gg_sum = [jnp.zeros((1, LANES), f32) for c in range(C)]
    for k in range(K):
        lo, hi, R = offs[k], offs[k + 1], rows[k]
        for c in range(C):
            @pl.when(not_mine(k, c))
            def _(k=k, c=c):
                B = blocks[k]
                pltpu.make_async_copy(part.at[k, c, 0:B], ag.at[k, c, 0:B], ag_recv.at[k, c]).wait()
        for c in range(C):
            cols = slice(c * LANES, (c + 1) * LANES)
            blk = ag[k, c, 0:R]
            gw[lo:hi, cols] = blk
            gg_sum[c] = gg_sum[c] + jnp.sum(blk * w[lo:hi, cols].astype(f32), axis=0, keepdims=True)
    for c in range(C):
        cols = slice(c * LANES, (c + 1) * LANES)
        gg[:, cols] = gg_sum[c] / gain_row[:, cols]
    last = rows[-1]
    gb[...] = ag[K - 1, 0, last:last + 1][:, 0:V]
    total = jnp.sum(ag[K - 1, 0, last + 1:last + 2], axis=1, keepdims=True)
    loss[...] = total / (factor * V * lat_total)

    @pl.loop(1, G)
    def _(i):
        lat_copy(i).wait_send()

    for i in range(1, M):
        for j in range(J):
            pred_copy(i, 0, points(j), ps_first.at[i, j], pr_first.at[i, j]).wait_send()
        for k in range(1, K):
            pred_copy(i, k, whole, ps.at[i, k], pr.at[i, k]).wait_send()
    for k in range(K):
        for c in range(C):
            @pl.when(not_mine(k, c))
            def _(k=k, c=c):
                rs_copy(k, c).wait_send()

        @pl.when(jnp.logical_and(is_owner, my_k == k))
        def _(k=k):
            @pl.loop(1, N)
            def _(i):
                ag_copy(k, i).wait_send()

    @pl.loop(0, J)
    def _(j):
        out_copy(j).wait()


def shards(fields, observed, lat_weight, var_weight, weight, bias, gain):
    G = lax.axis_size("grid")
    M = lax.axis_size("member")
    N = G * M
    V, PTS = observed.shape
    D = weight.shape[1]
    VP = -(-V // LANES) * LANES
    assert fields.shape[0] == 1 and PTS % POINT_BLOCK == 0 and VP == LANES
    K, offs, rows, blocks, C, per, S = plan(G, M, V, D)
    B = max(blocks)
    J = PTS // POINT_BLOCK
    vmem = pl.BlockSpec(memory_space=pltpu.VMEM)
    hbm = pl.BlockSpec(memory_space=pl.ANY)
    dma = pltpu.SemaphoreType.DMA
    gf, gw, gg, gb, loss = pl.pallas_call(
        functools.partial(body, G, M),
        out_shape=(
            jax.ShapeDtypeStruct(fields.shape, bf16),
            jax.ShapeDtypeStruct((V, D), f32),
            jax.ShapeDtypeStruct((1, D), f32),
            jax.ShapeDtypeStruct((1, V), f32),
            jax.ShapeDtypeStruct((1, 1), f32),
        ),
        in_specs=[hbm] + [vmem] * 6,
        out_specs=(hbm, vmem, vmem, vmem, vmem),
        scratch_shapes=[
            pltpu.VMEM((PTS, D), bf16),
            pltpu.VMEM((PTS, D), f32),
            pltpu.VMEM((PTS, D), bf16),
            pltpu.VMEM((PTS, 1), f32),
            pltpu.VMEM((PTS, D), bf16),
            pltpu.VMEM((VP, D), bf16),
            pltpu.VMEM((VP, PTS), bf16),
            pltpu.VMEM((VP, PTS), f32),
            pltpu.VMEM((M, VP, PTS), f32),
            pltpu.VMEM((8, LANES), f32),
            pltpu.VMEM((G, 8, LANES), f32),
            pltpu.VMEM((K, C, B, LANES), f32),
            pltpu.VMEM((N, B, LANES), f32),
            pltpu.VMEM((B, LANES), f32),
            pltpu.VMEM((K, C, B, LANES), f32),
            pltpu.VMEM((1, PTS), f32),
            dma((J,)), dma((J,)), dma((G,)), dma((G,)),
            dma((M, J)), dma((M, J)), dma((M, K)), dma((M, K)),
            dma((K, C)), dma((N,)), dma((N,)), dma((K, C)),
        ],
        compiler_params=pltpu.CompilerParams(collective_id=0, has_side_effects=True),
        name="crps_step",
    )(fields, observed, lat_weight[None, :], var_weight[None, :], weight, bias[None, :], gain[None, :])
    return gf, gw, gg.reshape(D), gb.reshape(V), loss.reshape(())


def solution(mesh):
    return jax.shard_map(
        shards,
        mesh=mesh,
        in_specs=(P("member", "grid", None), P(None, "grid"), P("grid"), P(), P(), P(), P()),
        out_specs=(P("member", "grid", None), P(), P(), P(), P()),
        check_vma=False,
    )
```

time: 168 us -> 50.6 us (0.30)
  blocking collectives: 83.1 us -> 0 us
  Pallas kernels: 0 us -> 42.6 us
  waiting for transfers between devices: 36.9 us -> 0 us
  between operations: 18.6 us -> 2.41 us
  other arithmetic: 13.8 us -> 0 us
  matrix products: 6.7 us -> 0 us
  local copies, waits for them, and re-layouts: 7.56 us -> 5 us
    psum x2 -> x0, blocking collectives: 70.8 us -> none  [the longest x1 39.6 us: shards(): lax.psum((part_weight, part_gain, part_bias, loss_part), ('grid', 'member'))]
    pallas_call x0 -> x1, Pallas kernels: none -> 42.6 us  [shards(): pl.pallas_call(functools.partial(body, G, M), out_shape=(jax.ShapeDtypeSt...]
    psum x1 -> x0, waiting for transfers between devices: 36.9 us -> none  [shards(): lax.psum((part_weight, part_gain, part_bias, loss_part), ('grid', 'member'))]
    all_gather x1 -> x0, blocking collectives: 12.3 us -> none  [shards(): everyone = lax.all_gather(predicted, 'member', axis=0, tiled=True)]
    dot_general x3 -> x0, matrix products: 6.7 us -> none  [the longest x1 4.23 us: shards(): jnp.einsum('rvp,vd->rpd', grad_pred, weight, preferred_element_type=jnp.f...]
    reduce_sum x7 -> x0, other arithmetic: 6.03 us -> none  [the longest x1 2.55 us: shards(): mean_one = jnp.mean(grad_unit, axis=-1, keepdims=True)]
    convert_element_type x2 -> x0, other arithmetic: 4.84 us -> none  [the longest x1 4.84 us: shards(): (factor * (inv_std * (grad_unit - mean_one - unit_rows * mean_two))).asty...]
    mul x3 -> x0, other arithmetic: 2.91 us -> none  [the longest x1 1.8 us: shards(): factor * grad_weight]
  transfers between devices with their start and end apart: 1 -> 0, of which waited for: 1 -> 0; matrix products, arithmetic and copies ran while one was open for 11% -> 0% of each run, Pallas kernels for 0% -> 0%
where the time goes in v1:
time: 50.6 us; the launch traced here: 50 us
  Pallas kernels  42.6 us (84%)
  local copies, waits for them, and re-layouts  5 us (10%)
  between operations  2.41 us (5%)
    pallas_call x1, Pallas kernels, shards(): pl.pallas_call(functools.partial(body, G, M), out_shape=(jax.ShapeDtypeSt...  42.6 us
    unnamed x10, local copies, waits for them, and re-layouts  5 us

profile of v1, /device:TPU:1, one launch (start us, length us, event | category | flops | bytes accessed | tf_op | source)
XLA Modules:
  0.0 50.0 jit_solution(11590379065669021633)
XLA Ops:
  0.6 42.6 %crps_step.1 = (bf16[1,1024,1024]{2,1,0:T(8,128)(2,1)}, f32[100,1024]{1,0:T(8,128)}, f32[1,1024]{1,0:T(1,128)}, f32[1,100]{1,0:T(1,128)}, f32[1,1]{1,0:T(1,128)}) custom-call(bf16[1,1024,1024]{2,1,0:T(8,128)(2,1)} %fields.1, bf16[100,1024]{1,0:T(8,128)(2,1)} %obs.1, f32[1,1024]{1,0:T(1,128)} %bitcast.7, f32[1,100]{1,0:T(1,128)} %bitcast.10, ...), custom_call_target="tpu_custom_call" | custom-call | tf_op jit(solution)/shard_map/crps_step/pallas_call | solution.py:301
  43.2 0.0 copy-start
  43.2 0.0 copy-start.1
  43.3 0.0 copy-start.2
  43.3 3.1 %copy.17 = bf16[1,1024,1024]{2,1,0:T(8,128)(2,1)} copy(bf16[1,1024,1024]{2,1,0:T(8,128)(2,1)} %get-tuple-element.20) | data formatting | bytes 4194304
  46.4 0.0 copy-done
  46.4 0.8 %copy.18 = f32[100,1024]{1,0:T(8,128)} copy(f32[100,1024]{1,0:T(8,128)S(1)} %copy-done) | data formatting | bytes 819200
  47.2 0.0 copy-done.1
  47.2 0.6 %copy.19 = f32[1024]{0:T(1024)} copy(f32[1024]{0:T(1024)S(1)} %bitcast.9) | data formatting | bytes 8192
  47.8 0.0 copy-done.2
  47.8 0.5 %copy.20 = f32[100]{0:T(128)} copy(f32[100]{0:T(128)S(1)} %bitcast.12) | data formatting | bytes 800
Async XLA Ops:
  43.2 3.2 %copy-start = (f32[100,1024]{1,0:T(8,128)S(1)}, f32[100,1024]{1,0:T(8,128)}, u32[]{:S(2)}) copy-start(f32[100,1024]{1,0:T(8,128)} %get-tuple-element.21) | copy-start | bytes 1228804
  43.2 3.9 %copy-start.1 = (f32[1,1024]{1,0:T(1,128)S(1)}, f32[1,1024]{1,0:T(1,128)}, u32[]{:S(2)}) copy-start(f32[1,1024]{1,0:T(1,128)} %get-tuple-element.12) | copy-start | bytes 12292
  43.3 4.5 %copy-start.2 = (f32[1,100]{1,0:T(1,128)S(1)}, f32[1,100]{1,0:T(1,128)}, u32[]{:S(2)}) copy-start(f32[1,100]{1,0:T(1,128)} %get-tuple-element.13) | copy-start | bytes 1204

commit v2 on v1

--- a/solution.py
+++ b/solution.py
@@ -24,10 +24,10 @@
     rows = [offs[k + 1] - offs[k] for k in range(K)]
     extra = -(-(rows[-1] + 2) // 8) * 8
     blocks = rows[:-1] + [extra]
-    C = D // LANES
-    per = G // K
+    C = D // LANES // 2
+    per = G // 2 // K
     S = (M * per) // C
-    assert G % K == 0 and (M * per) % C == 0 and S >= 1
+    assert G % (2 * K) == 0 and D % (2 * LANES) == 0 and (M * per) % C == 0 and S >= 1
     return K, offs, rows, blocks, C, per, S
 
 
@@ -39,28 +39,35 @@
 
 def body(G, M, fields, obs, lat, vw, w, bias, gain,
          gf, gw, gg, gb, loss,
-         x, unit, normed, inv, outb, wp, gp, pred, others, lat_own, lat_all,
-         part, rs, ag_src, ag, lossb,
-         in_sem, out_sem, lat_send, lat_recv, ps_first, pr_first, ps, pr,
-         rs_send, rs_recv, ag_send, ag_recv):
+         x, unit, normed, inv, outb, wp, gp, pred, others, lat_own, lat_sib, lat_all,
+         part, sib, rs, ag_src, ag, lossb,
+         in_sem, out_sem, lat_pair, lat_send, lat_recv, ps, pr, sib_send, sib_recv,
+         rs_send, rs_recv, ag_send, ag_recv, fw_send, fw_recv):
     V, PTS = obs.shape
     D = w.shape[1]
     VP = wp.shape[0]
-    N = G * M
+    H = G // 2
+    N = H * M
     K, offs, rows, blocks, C, per, S = plan(G, M, V, D)
     ends = [-(-hi // 8) * 8 for hi in offs[1:]]
     J = PTS // POINT_BLOCK
     g = lax.axis_index("grid")
     m = lax.axis_index("member")
-    me = m * G + g
-    my_k = lax.rem(g, K)
-    my_cf = m * per + g // K
+    q = lax.rem(g, 2)
+    h = g // 2
+    me = m * H + h
+    my_k = lax.rem(h, K)
+    my_cf = m * per + h // K
     my_c = my_cf // S
+    mine = q * C
+    theirs = (1 - q) * C
+    sibling = {"grid": g + 1 - 2 * q, "member": m}
 
     def device(t):
-        return {"grid": lax.rem(t, G), "member": t // G}
+        return {"grid": lax.rem(t, H) * 2 + q, "member": t // H}
 
     barrier = pltpu.get_barrier_semaphore()
+    pl.semaphore_signal(barrier, inc=1, device_id=sibling, device_id_type=MESH_ID)
 
     @pl.loop(1, N)
     def _(i):
@@ -79,20 +86,19 @@
     bias_col = to_column(bias[...], VP)
     vw_col = to_column(vw[...], VP)
     gain_row = gain[...]
-    pl.semaphore_wait(barrier, N - 1)
+
+    def lat_sibling():
+        return pltpu.make_async_remote_copy(
+            lat_own, lat_sib, lat_pair.at[0], lat_pair.at[1], device_id=sibling, device_id_type=MESH_ID)
 
     def lat_copy(i):
         return pltpu.make_async_remote_copy(
-            lat_own, lat_all.at[g], lat_send.at[i], lat_recv.at[g],
-            device_id={"grid": lax.rem(g + i, G), "member": m}, device_id_type=MESH_ID)
-
-    @pl.loop(1, G)
-    def _(i):
-        lat_copy(i).start()
-
-    def pred_copy(i, k, at, send, recv):
-        return pltpu.make_async_remote_copy(
-            pred.at[offs[k]:ends[k], at], others.at[i, offs[k]:ends[k], at], send, recv,
+            lat_all.at[h], lat_all.at[h], lat_send.at[i], lat_recv.at[h],
+            device_id={"grid": lax.rem(h + i, H) * 2 + q, "member": m}, device_id_type=MESH_ID)
+
+    def pred_copy(i, k):
+        return pltpu.make_async_remote_copy(
+            pred.at[offs[k]:ends[k]], others.at[i, offs[k]:ends[k]], ps.at[i, k], pr.at[i, k],
             device_id={"grid": g, "member": lax.rem(m + i, M)}, device_id_type=MESH_ID)
 
     def points(j):
@@ -113,49 +119,53 @@
         p = lax.dot_general(wp[...], normed[points(j), :], (((1,), (1,)), ((), ())),
                             preferred_element_type=f32)
         pred[:, points(j)] = p + bias_col
+
+    pl.semaphore_wait(barrier, N)
+    for k in range(K):
         for i in range(1, M):
-            pred_copy(i, 0, points(j), ps_first.at[i, j], pr_first.at[i, j]).start()
-
-    whole = slice(0, PTS)
-    for k in range(1, K):
-        for i in range(1, M):
-            pred_copy(i, k, whole, ps.at[i, k], pr.at[i, k]).start()
-
-    lat_all[g] = lat_own[...]
-
-    @pl.loop(1, G)
+            pred_copy(i, k).start()
+    lat_sibling().start()
+
+    lat_sibling().wait()
+    lat_all[h] = lat_own[...] + lat_sib[...]
+
+    @pl.loop(1, H)
     def _(i):
-        src = lax.rem(g + i, G)
-        pltpu.make_async_copy(lat_own, lat_all.at[src], lat_recv.at[src]).wait()
-
-    lat_total = jnp.sum(lat_all[...], axis=0)[0:1, 0:1]
-    factor = (PTS * G) / lat_total
+        lat_copy(i).start()
+
+    def lat_all_wait():
+        @pl.loop(1, H)
+        def _(i):
+            src = lax.rem(h + i, H)
+            pltpu.make_async_copy(lat_own, lat_all.at[src], lat_recv.at[src]).wait()
 
     scale_pair = 1.0 / (M * (M - 1))
     lossb[...] = jnp.zeros(lossb.shape, f32)
     ones = jnp.ones((8, PTS), bf16)
 
-    def unit_device(k, c):
+    def unit_owner(k, c):
         cf = c * S
         return cf // per, (cf % per) * K + k
 
+    def sib_copy(k):
+        B = blocks[k]
+        return pltpu.make_async_remote_copy(
+            part.at[k, pl.ds(theirs, C), 0:B], sib.at[k, :, 0:B], sib_send.at[k], sib_recv.at[k],
+            device_id=sibling, device_id_type=MESH_ID)
+
     def rs_copy(k, c):
-        om, og = unit_device(k, c)
-        return pltpu.make_async_remote_copy(
-            part.at[k, c, 0:blocks[k]], rs.at[me, 0:blocks[k]], rs_send.at[k, c], rs_recv.at[me],
-            device_id={"grid": og, "member": om}, device_id_type=MESH_ID)
+        om, oh = unit_owner(k, c)
+        return pltpu.make_async_remote_copy(
+            part.at[k, mine + c, 0:blocks[k]], rs.at[me, 0:blocks[k]], rs_send.at[k, c], rs_recv.at[me],
+            device_id={"grid": oh * 2 + q, "member": om}, device_id_type=MESH_ID)
 
     def not_mine(k, c):
-        om, og = unit_device(k, c)
-        return jnp.logical_or(m != om, g != og)
+        om, oh = unit_owner(k, c)
+        return jnp.logical_or(m != om, h != oh)
 
     for k in range(K):
         for i in range(1, M):
-            if k == 0:
-                for j in range(J):
-                    pred_copy(i, 0, points(j), ps_first.at[i, j], pr_first.at[i, j]).wait_recv()
-            else:
-                pred_copy(i, k, whole, ps.at[i, k], pr.at[i, k]).wait_recv()
+            pred_copy(i, k).wait_recv()
         lo, hi, R = offs[k], offs[k + 1], rows[k]
         own = pred[lo:hi, :]
         e = own - obs[lo:hi, :].astype(f32)
@@ -179,22 +189,30 @@
             lane = jnp.zeros((1, LANES), f32)
             for j in range(PTS // LANES):
                 lane = lane + lossb[:, j * LANES:(j + 1) * LANES]
-        for c in range(C):
+        for c in range(2 * C):
             part[k, c, 0:R] = gwk[:, c * LANES:(c + 1) * LANES]
             if k == K - 1:
                 part[k, c, R:R + 1] = gbp[0:1, :]
                 part[k, c, R + 1:R + 2] = lane
                 if blocks[k] > R + 2:
                     part[k, c, R + 2:blocks[k]] = jnp.zeros((blocks[k] - R - 2, LANES), f32)
-        for c in range(C):
+        sib_copy(k).start()
+        sib_copy(k).wait_recv()
+        for c in range(C):
+            part[k, mine + c, 0:blocks[k]] += sib[k, c, 0:blocks[k]]
+
             @pl.when(not_mine(k, c))
             def _(k=k, c=c):
                 rs_copy(k, c).start()
 
+    lat_all_wait()
+    lat_total = jnp.sum(lat_all[...], axis=0)[0:1, 0:1]
+    factor = (PTS * G) / lat_total
+
     def ag_copy(k, i):
         B = blocks[k]
         return pltpu.make_async_remote_copy(
-            ag_src.at[0:B], ag.at[k, my_c, 0:B], ag_send.at[i], ag_recv.at[k, my_c],
+            ag_src.at[0:B], ag.at[k, mine + my_c, 0:B], ag_send.at[i], ag_recv.at[k, my_c],
             device_id=device(lax.rem(me + i, N)), device_id_type=MESH_ID)
 
     is_owner = lax.rem(my_cf, S) == 0
@@ -209,9 +227,9 @@
                 pltpu.make_async_copy(part.at[k, 0, 0:B], rs.at[src, 0:B], rs_recv.at[src]).wait()
                 return acc + rs[src, 0:B]
 
-            acc = lax.fori_loop(1, N, add, part[k, my_c, 0:B]) * factor
+            acc = lax.fori_loop(1, N, add, part[k, mine + my_c, 0:B]) * factor
             ag_src[0:B] = acc
-            ag[k, my_c, 0:B] = acc
+            ag[k, mine + my_c, 0:B] = acc
 
             @pl.loop(1, N)
             def _(i):
@@ -237,20 +255,31 @@
         reduce_and_spread(k)
     pl.loop(J // 2, J)(grad_block)
 
-    gg_sum = [jnp.zeros((1, LANES), f32) for c in range(C)]
-    for k in range(K):
-        lo, hi, R = offs[k], offs[k + 1], rows[k]
+    def fw_copy(k, c):
+        B = blocks[k]
+        return pltpu.make_async_remote_copy(
+            ag.at[k, mine + c, 0:B], ag.at[k, mine + c, 0:B], fw_send.at[k, c], fw_recv.at[k, c],
+            device_id=sibling, device_id_type=MESH_ID)
+
+    for k in range(K):
         for c in range(C):
             @pl.when(not_mine(k, c))
             def _(k=k, c=c):
                 B = blocks[k]
-                pltpu.make_async_copy(part.at[k, c, 0:B], ag.at[k, c, 0:B], ag_recv.at[k, c]).wait()
-        for c in range(C):
+                pltpu.make_async_copy(part.at[k, 0, 0:B], ag.at[k, mine + c, 0:B], ag_recv.at[k, c]).wait()
+            fw_copy(k, c).start()
+    gg_sum = [jnp.zeros((1, LANES), f32) for c in range(2 * C)]
+    for k in range(K):
+        lo, hi, R = offs[k], offs[k + 1], rows[k]
+        for c in range(C):
+            B = blocks[k]
+            pltpu.make_async_copy(part.at[k, 0, 0:B], ag.at[k, theirs + c, 0:B], fw_recv.at[k, c]).wait()
+        for c in range(2 * C):
             cols = slice(c * LANES, (c + 1) * LANES)
             blk = ag[k, c, 0:R]
             gw[lo:hi, cols] = blk
             gg_sum[c] = gg_sum[c] + jnp.sum(blk * w[lo:hi, cols].astype(f32), axis=0, keepdims=True)
-    for c in range(C):
+    for c in range(2 * C):
         cols = slice(c * LANES, (c + 1) * LANES)
         gg[:, cols] = gg_sum[c] / gain_row[:, cols]
     last = rows[-1]
@@ -258,16 +287,16 @@
     total = jnp.sum(ag[K - 1, 0, last + 1:last + 2], axis=1, keepdims=True)
     loss[...] = total / (factor * V * lat_total)
 
-    @pl.loop(1, G)
+    @pl.loop(1, H)
     def _(i):
         lat_copy(i).wait_send()
 
-    for i in range(1, M):
-        for j in range(J):
-            pred_copy(i, 0, points(j), ps_first.at[i, j], pr_first.at[i, j]).wait_send()
-        for k in range(1, K):
-            pred_copy(i, k, whole, ps.at[i, k], pr.at[i, k]).wait_send()
-    for k in range(K):
+    for k in range(K):
+        for i in range(1, M):
+            pred_copy(i, k).wait_send()
+        sib_copy(k).wait_send()
+        for c in range(C):
+            fw_copy(k, c).wait_send()
         for c in range(C):
             @pl.when(not_mine(k, c))
             def _(k=k, c=c):
@@ -287,7 +316,8 @@
 def shards(fields, observed, lat_weight, var_weight, weight, bias, gain):
     G = lax.axis_size("grid")
     M = lax.axis_size("member")
-    N = G * M
+    H = G // 2
+    N = H * M
     V, PTS = observed.shape
     D = weight.shape[1]
     VP = -(-V // LANES) * LANES
@@ -320,15 +350,17 @@
             pltpu.VMEM((VP, PTS), f32),
             pltpu.VMEM((M, VP, PTS), f32),
             pltpu.VMEM((8, LANES), f32),
-            pltpu.VMEM((G, 8, LANES), f32),
+            pltpu.VMEM((8, LANES), f32),
+            pltpu.VMEM((H, 8, LANES), f32),
+            pltpu.VMEM((K, 2 * C, B, LANES), f32),
             pltpu.VMEM((K, C, B, LANES), f32),
             pltpu.VMEM((N, B, LANES), f32),
             pltpu.VMEM((B, LANES), f32),
-            pltpu.VMEM((K, C, B, LANES), f32),
+            pltpu.VMEM((K, 2 * C, B, LANES), f32),
             pltpu.VMEM((1, PTS), f32),
-            dma((J,)), dma((J,)), dma((G,)), dma((G,)),
-            dma((M, J)), dma((M, J)), dma((M, K)), dma((M, K)),
-            dma((K, C)), dma((N,)), dma((N,)), dma((K, C)),
+            dma((J,)), dma((J,)), dma((2,)), dma((H,)), dma((H,)),
+            dma((M, K)), dma((M, K)), dma((K,)), dma((K,)),
+            dma((K, C)), dma((N,)), dma((N,)), dma((K, C)), dma((K, C)), dma((K, C)),
         ],
         compiler_params=pltpu.CompilerParams(collective_id=0, has_side_effects=True),
         name="crps_step",

time: 50.6 us -> 43.7 us (0.86)
  Pallas kernels: 42.6 us -> 36.1 us
    pallas_call x1, Pallas kernels: 42.6 us -> 36.1 us  [shards(): pl.pallas_call(functools.partial(body, G, M), out_shape=(jax.ShapeDtypeSt...]
where the time goes in v2:
time: 43.7 us; the launch traced here: 43.5 us
  Pallas kernels  36.1 us (83%)
  local copies, waits for them, and re-layouts  5 us (11%)
  between operations  2.41 us (6%)
    pallas_call x1, Pallas kernels, shards(): pl.pallas_call(functools.partial(body, G, M), out_shape=(jax.ShapeDtypeSt...  36.1 us
    unnamed x10, local copies, waits for them, and re-layouts  5 us

profile of v2, /device:TPU:1, one launch (start us, length us, event | category | flops | bytes accessed | tf_op | source)
XLA Modules:
  0.0 43.5 jit_solution(16265201669067668471)
XLA Ops:
  0.6 36.1 %crps_step.1 = (bf16[1,1024,1024]{2,1,0:T(8,128)(2,1)}, f32[100,1024]{1,0:T(8,128)}, f32[1,1024]{1,0:T(1,128)}, f32[1,100]{1,0:T(1,128)}, f32[1,1]{1,0:T(1,128)}) custom-call(bf16[1,1024,1024]{2,1,0:T(8,128)(2,1)} %fields.1, bf16[100,1024]{1,0:T(8,128)(2,1)} %obs.1, f32[1,1024]{1,0:T(1,128)} %bitcast.7, f32[1,100]{1,0:T(1,128)} %bitcast.10, ...), custom_call_target="tpu_custom_call" | custom-call | tf_op jit(solution)/shard_map/crps_step/pallas_call | solution.py:331
  36.7 0.0 copy-start
  36.7 0.0 copy-start.1
  36.7 0.0 copy-start.2
  36.7 3.1 %copy.17 = bf16[1,1024,1024]{2,1,0:T(8,128)(2,1)} copy(bf16[1,1024,1024]{2,1,0:T(8,128)(2,1)} %get-tuple-element.20) | data formatting | bytes 4194304
  39.9 0.0 copy-done
  39.9 0.8 %copy.18 = f32[100,1024]{1,0:T(8,128)} copy(f32[100,1024]{1,0:T(8,128)S(1)} %copy-done) | data formatting | bytes 819200
  40.6 0.0 copy-done.1
  40.6 0.6 %copy.19 = f32[1024]{0:T(1024)} copy(f32[1024]{0:T(1024)S(1)} %bitcast.9) | data formatting | bytes 8192
  41.2 0.0 copy-done.2
  41.2 0.5 %copy.20 = f32[100]{0:T(128)} copy(f32[100]{0:T(128)S(1)} %bitcast.12) | data formatting | bytes 800
Async XLA Ops:
  36.7 3.2 %copy-start = (f32[100,1024]{1,0:T(8,128)S(1)}, f32[100,1024]{1,0:T(8,128)}, u32[]{:S(2)}) copy-start(f32[100,1024]{1,0:T(8,128)} %get-tuple-element.21) | copy-start | bytes 1228804
  36.7 3.9 %copy-start.1 = (f32[1,1024]{1,0:T(1,128)S(1)}, f32[1,1024]{1,0:T(1,128)}, u32[]{:S(2)}) copy-start(f32[1,1024]{1,0:T(1,128)} %get-tuple-element.12) | copy-start | bytes 12292
  36.7 4.5 %copy-start.2 = (f32[1,100]{1,0:T(1,128)S(1)}, f32[1,100]{1,0:T(1,128)}, u32[]{:S(2)}) copy-start(f32[1,100]{1,0:T(1,128)} %get-tuple-element.13) | copy-start | bytes 1204

commit v3 on v2

--- a/solution.py
+++ b/solution.py
@@ -39,9 +39,9 @@
 
 def body(G, M, fields, obs, lat, vw, w, bias, gain,
          gf, gw, gg, gb, loss,
-         x, unit, normed, inv, outb, wp, gp, pred, others, lat_own, lat_sib, lat_all,
+         x, unit, normed, inv, wp, gp, pred, others, lat_own, lat_sib, lat_all,
          part, sib, rs, ag_src, ag, lossb,
-         in_sem, out_sem, lat_pair, lat_send, lat_recv, ps, pr, sib_send, sib_recv,
+         in_sem, lat_pair, lat_send, lat_recv, ps, pr, sib_send, sib_recv,
          rs_send, rs_recv, ag_send, ag_recv, fw_send, fw_recv):
     V, PTS = obs.shape
     D = w.shape[1]
@@ -235,9 +235,6 @@
             def _(i):
                 ag_copy(k, i).start()
 
-    def out_copy(j):
-        return pltpu.make_async_copy(outb.at[points(j)], gf.at[0, points(j)], out_sem.at[j])
-
     def grad_block(j):
         gn = lax.dot_general(gp[:, points(j)], wp[...], (((0,), (0,)), ((), ())),
                              preferred_element_type=f32)
@@ -245,8 +242,7 @@
         u = unit[points(j), :]
         one = jnp.mean(gu, axis=-1, keepdims=True)
         two = jnp.mean(gu * u, axis=-1, keepdims=True)
-        outb[points(j), :] = ((factor * inv[points(j), :]) * (gu - one - u * two)).astype(bf16)
-        out_copy(j).start()
+        gf[points(j), :] = ((factor * inv[points(j), :]) * (gu - one - u * two)).astype(bf16)
 
     for k in range(K - 2):
         reduce_and_spread(k)
@@ -308,9 +304,15 @@
             def _(i):
                 ag_copy(k, i).wait_send()
 
-    @pl.loop(0, J)
-    def _(j):
-        out_copy(j).wait()
+
+def write_out(*refs):
+    n = len(refs) // 2
+    sem = refs[-1]
+    copies = [pltpu.make_async_copy(refs[i], refs[n + i], sem.at[i]) for i in range(n)]
+    for copy in copies:
+        copy.start()
+    for copy in copies:
+        copy.wait()
 
 
 def shards(fields, observed, lat_weight, var_weight, weight, bias, gain):
@@ -328,23 +330,22 @@
     vmem = pl.BlockSpec(memory_space=pltpu.VMEM)
     hbm = pl.BlockSpec(memory_space=pl.ANY)
     dma = pltpu.SemaphoreType.DMA
-    gf, gw, gg, gb, loss = pl.pallas_call(
+    held = pl.pallas_call(
         functools.partial(body, G, M),
         out_shape=(
-            jax.ShapeDtypeStruct(fields.shape, bf16),
-            jax.ShapeDtypeStruct((V, D), f32),
-            jax.ShapeDtypeStruct((1, D), f32),
-            jax.ShapeDtypeStruct((1, V), f32),
-            jax.ShapeDtypeStruct((1, 1), f32),
+            pltpu.VMEM((PTS, D), bf16),
+            pltpu.VMEM((V, D), f32),
+            pltpu.VMEM((1, D), f32),
+            pltpu.VMEM((1, V), f32),
+            pltpu.VMEM((1, 1), f32),
         ),
         in_specs=[hbm] + [vmem] * 6,
-        out_specs=(hbm, vmem, vmem, vmem, vmem),
+        out_specs=(vmem,) * 5,
         scratch_shapes=[
             pltpu.VMEM((PTS, D), bf16),
             pltpu.VMEM((PTS, D), f32),
             pltpu.VMEM((PTS, D), bf16),
             pltpu.VMEM((PTS, 1), f32),
-            pltpu.VMEM((PTS, D), bf16),
             pltpu.VMEM((VP, D), bf16),
             pltpu.VMEM((VP, PTS), bf16),
             pltpu.VMEM((VP, PTS), f32),
@@ -358,14 +359,22 @@
             pltpu.VMEM((B, LANES), f32),
             pltpu.VMEM((K, 2 * C, B, LANES), f32),
             pltpu.VMEM((1, PTS), f32),
-            dma((J,)), dma((J,)), dma((2,)), dma((H,)), dma((H,)),
+            dma((J,)), dma((2,)), dma((H,)), dma((H,)),
             dma((M, K)), dma((M, K)), dma((K,)), dma((K,)),
             dma((K, C)), dma((N,)), dma((N,)), dma((K, C)), dma((K, C)), dma((K, C)),
         ],
         compiler_params=pltpu.CompilerParams(collective_id=0, has_side_effects=True),
         name="crps_step",
     )(fields, observed, lat_weight[None, :], var_weight[None, :], weight, bias[None, :], gain[None, :])
-    return gf, gw, gg.reshape(D), gb.reshape(V), loss.reshape(())
+    gf, gw, gg, gb, loss = pl.pallas_call(
+        write_out,
+        out_shape=tuple(jax.ShapeDtypeStruct(a.shape, a.dtype) for a in held),
+        in_specs=[vmem] * 5,
+        out_specs=(hbm,) * 5,
+        scratch_shapes=[dma((5,))],
+        name="write_out",
+    )(*[pltpu.with_memory_space_constraint(a, pltpu.VMEM) for a in held])
+    return gf.reshape(fields.shape), gw, gg.reshape(D), gb.reshape(V), loss.reshape(())
 
 
 def solution(mesh):

time: 43.7 us -> 38.7 us (0.89)
  local copies, waits for them, and re-layouts: 5 us -> 0 us
  between operations: 2.41 us -> 0.64 us
  Pallas kernels: 36.1 us -> 37.8 us
    unnamed x10 -> x0, local copies, waits for them, and re-layouts: 5 us -> none
    pallas_call x1 -> x2, Pallas kernels: 36.1 us -> 37.8 us  [the longest x1 35.7 us: shards(): pl.pallas_call(functools.partial(body, G, M), out_shape=(pltpu.VMEM((PTS,...]
where the time goes in v3:
time: 38.7 us; the launch traced here: 38.5 us
  Pallas kernels  37.8 us (98%)
  between operations  0.64 us (2%)
    pallas_call x1, Pallas kernels, shards(): pl.pallas_call(functools.partial(body, G, M), out_shape=(pltpu.VMEM((PTS,...  35.7 us
    pallas_call x1, Pallas kernels, shards(): pl.pallas_call(write_out, out_shape=tuple((jax.ShapeDtypeStruct(a.shape,...  2.13 us

profile of v3, /device:TPU:1, one launch (start us, length us, event | category | flops | bytes accessed | tf_op | source)
XLA Modules:
  0.0 38.5 jit_solution(10337869452998027205)
XLA Ops:
  0.6 35.7 %crps_step.1 = (bf16[1024,1024]{1,0:T(8,128)(2,1)S(1)}, f32[100,1024]{1,0:T(8,128)S(1)}, f32[1,1024]{1,0:T(1,128)S(1)}, f32[1,100]{1,0:T(1,128)S(1)}, f32[1,1]{1,0:T(1,128)}) custom-call(bf16[1,1024,1024]{2,1,0:T(8,128)(2,1)} %fields.1, bf16[100,1024]{1,0:T(8,128)(2,1)} %obs.1, f32[1,1024]{1,0:T(1,128)} %bitcast.8, f32[1,100]{1,0:T(1,128)} %bitcast.10, ...), custom_call_target="tpu_custom_call" | custom-call | tf_op jit(solution)/shard_map/crps_step/pallas_call | solution.py:333
  36.4 2.1 %write_out.1 = (bf16[1024,1024]{1,0:T(8,128)(2,1)}, f32[100,1024]{1,0:T(8,128)}, f32[1,1024]{1,0:T(1,128)}, f32[1,100]{1,0:T(1,128)}, f32[1,1]{1,0:T(1,128)}) custom-call(bf16[1024,1024]{1,0:T(8,128)(2,1)S(1)} %get-tuple-element.15.refs_0_, f32[100,1024]{1,0:T(8,128)S(1)} %get-tuple-element.16.refs_1_, f32[1,1024]{1,0:T(1,128)S(1)} %get-tuple-element.17.refs_2_, ...), custom_call_target="tpu_custom_call" | custom-call | tf_op jit(solution)/shard_map/write_out/pallas_call | solution.py:369

commit v4 on v3

--- a/solution.py
+++ b/solution.py
@@ -20,7 +20,7 @@
 
 def plan(G, M, V, D):
     K = ROW_CHUNKS
-    offs = [int(V * k / K / 16 + 0.5) * 16 for k in range(K)] + [V]
+    offs = [-(-V * k // (16 * K)) * 16 for k in range(K)] + [V]
     rows = [offs[k + 1] - offs[k] for k in range(K)]
     extra = -(-(rows[-1] + 2) // 8) * 8
     blocks = rows[:-1] + [extra]

time: 38.7 us -> 38.6 us (level)
  no operation moved by 1% of the time
where the time goes in v4:
time: 38.6 us; the launch traced here: 38.5 us
  Pallas kernels  37.8 us (98%)
  between operations  0.64 us (2%)
    pallas_call x1, Pallas kernels, shards(): pl.pallas_call(functools.partial(body, G, M), out_shape=(pltpu.VMEM((PTS,...  35.7 us
    pallas_call x1, Pallas kernels, shards(): pl.pallas_call(write_out, out_shape=tuple((jax.ShapeDtypeStruct(a.shape,...  2.13 us

profile of v4, /device:TPU:1, one launch (start us, length us, event | category | flops | bytes accessed | tf_op | source)
XLA Modules:
  0.0 38.5 jit_solution(610620691754607089)
XLA Ops:
  0.6 35.7 %crps_step.1 = (bf16[1024,1024]{1,0:T(8,128)(2,1)S(1)}, f32[100,1024]{1,0:T(8,128)S(1)}, f32[1,1024]{1,0:T(1,128)S(1)}, f32[1,100]{1,0:T(1,128)S(1)}, f32[1,1]{1,0:T(1,128)}) custom-call(bf16[1,1024,1024]{2,1,0:T(8,128)(2,1)} %fields.1, bf16[100,1024]{1,0:T(8,128)(2,1)} %obs.1, f32[1,1024]{1,0:T(1,128)} %bitcast.8, f32[1,100]{1,0:T(1,128)} %bitcast.10, ...), custom_call_target="tpu_custom_call" | custom-call | tf_op jit(solution)/shard_map/crps_step/pallas_call | solution.py:333
  36.3 2.1 %write_out.1 = (bf16[1024,1024]{1,0:T(8,128)(2,1)}, f32[100,1024]{1,0:T(8,128)}, f32[1,1024]{1,0:T(1,128)}, f32[1,100]{1,0:T(1,128)}, f32[1,1]{1,0:T(1,128)}) custom-call(bf16[1024,1024]{1,0:T(8,128)(2,1)S(1)} %get-tuple-element.15.refs_0_, f32[100,1024]{1,0:T(8,128)S(1)} %get-tuple-element.16.refs_1_, f32[1,1024]{1,0:T(1,128)S(1)} %get-tuple-element.17.refs_2_, ...), custom_call_target="tpu_custom_call" | custom-call | tf_op jit(solution)/shard_map/write_out/pallas_call | solution.py:369
